TPU v7x, 256 devices: a whole 4x4x8 slice. The times are simulated.
256 devices in a mesh: row: 32 (over x, z_lo, core), col: 8 (over z_hi, y).
Axes of the slice: x: 4, y: 4, z: 8 (z_hi: 2, z_lo: 4; z = z_hi * 4 + z_lo), core: 2. Of those that a mesh axis runs over, the one named last changes fastest.
Arguments:
- embed_first: bfloat16 [1536, 16384], P('col', 'row'), may hold values from -6 to 6
- embed_second: bfloat16 [1536, 16384], P('row', 'col'), may hold values from -6 to 6
- corr_grad: float32 [16384, 16384], P('row', 'col'), may hold values from -0.046875 to 0.046875
Outputs:
- grad_first: bfloat16 [1536, 16384], P('col', 'row')
- grad_second: bfloat16 [1536, 16384], P('row', 'col')
All inputs are finite; a program needn't handle non-finite values.
Results may differ from a plain program's by a relative error of at most 0.0065.
Values may be sent and summed in bfloat16 or wider, within the bound.
A program may use at most 128 MiB of HBM per device.

v0:
```python
import jax
import jax.numpy as jnp
from jax import lax
from jax.sharding import PartitionSpec as P


def cut_along(x, dim, peers):
    lengths = x.shape
    parts = x.reshape(*lengths[:dim], peers, lengths[dim] // peers, *lengths[dim + 1 :])
    return jnp.moveaxis(parts, dim, 0)


def sent_and_summed(x, axis, dim):
    peers = lax.axis_size(axis)
    parts = lax.all_to_all(cut_along(x, dim, peers), axis, 0, 0, tiled=True)
    return jnp.sum(parts.astype(jnp.float32), axis=0)


def local(embed_first, embed_second, corr_grad):
    low_grad = corr_grad.astype(jnp.bfloat16)
    first_terms = lax.dot_general(
        lax.all_gather(embed_second, "row", axis=0, tiled=True),
        low_grad,
        (((1,), (1,)), ((), ())),
        preferred_element_type=jnp.float32,
    )
    grad_first = sent_and_summed(first_terms.astype(jnp.bfloat16), "col", 0).astype(jnp.bfloat16)
    whole_first = lax.all_gather(embed_first, "col", axis=0, tiled=True)
    grad_second = sent_and_summed(
        jnp.dot(whole_first, low_grad, preferred_element_type=jnp.float32).astype(jnp.bfloat16),
        "row",
        0,
    ).astype(jnp.bfloat16)
    return (grad_first, grad_second)


def solution(mesh):
    return jax.shard_map(
        local,
        mesh=mesh,
        in_specs=(P("col", "row"), P("row", "col"), P("row", "col")),
        out_specs=(P("col", "row"), P("row", "col")),
        check_vma=False,
    )
```

profile of v0, /device:TPU:2, one launch (start us, length us, event | category | flops | bytes accessed | tf_op | source)
XLA Modules:
  0.0 316.0 jit_solution(858558997219356227)
XLA Ops:
  7.2 0.0 all-gather.5.cloned.1.call-start
  7.2 0.7 all-gather.5.cloned.1.call-update
  7.9 0.0 all-gather.3.cloned.1.call-start
  7.9 0.7 all-gather.3.cloned.1.call-update
  8.6 73.9 %all-gather.5.cloned.1.call-done = bf16[1536,512]{1,0:T(8,128)(2,1)} async-done(((bf16[192,512]{1,0:T(8,128)(2,1)}), bf16[1536,512]{1,0:T(8,128)(2,1)}) %all-gather.5.cloned.1.call-update) | async-done | bytes 1572880 | tf_op jit(solution)/shard_map/all_gather | solution.py:28
  82.6 8.8 %convolution_convert_fusion = bf16[1536,2048]{1,0:T(8,128)(2,1)} fusion(bf16[1536,512]{1,0:T(8,128)(2,1)} %all-gather.5.cloned.1.call-done, f32[512,2048]{1,0:T(8,128)} %param.5), kind=kOutput, calls=%fused_computation | convolution fusion | flops 3225419776 | bytes 12058624 | tf_op jit(solution)/shard_map/dot_general | solution.py:30
  91.3 5.3 %all-to-all-start.1 = ((bf16[32,48,2048]{2,1,0:T(8,128)(2,1)}), bf16[32,48,2048]{2,1,0:T(8,128)(2,1)}, u32[]{:S(2)}, u32[]{:S(2)}) async-start(bf16[32,48,2048]{2,1,0:T(8,128)(2,1)} %bitcast.4), calls=%async_computation.1 | async-start | bytes 12582912 | tf_op jit(solution)/shard_map/all_to_all | solution.py:15
  96.6 133.8 %all-gather.3.cloned.1.call-done = bf16[1536,2048]{1,0:T(8,128)(2,1)} async-done(((bf16[48,2048]{1,0:T(8,128)(2,1)}), bf16[1536,2048]{1,0:T(8,128)(2,1)}) %all-gather.3.cloned.1.call-update) | async-done | bytes 6291472 | tf_op jit(solution)/shard_map/all_gather | solution.py:22
  230.4 8.6 %convolution_convert_fusion.1 = bf16[1536,512]{1,0:T(8,128)(2,1)} fusion(bf16[1536,2048]{1,0:T(8,128)(2,1)} %all-gather.3.cloned.1.call-done, f32[512,2048]{1,0:T(8,128)} %param.5), kind=kOutput, calls=%fused_computation.1 | convolution fusion | flops 3223060480 | bytes 12058624 | tf_op jit(solution)/shard_map/dot_general | solution.py:21
  239.0 32.0 %all-to-all-done.1 = bf16[32,48,2048]{2,1,0:T(8,128)(2,1)} async-done(((bf16[32,48,2048]{2,1,0:T(8,128)(2,1)}), bf16[32,48,2048]{2,1,0:T(8,128)(2,1)}, u32[]{:S(2)}, u32[]{:S(2)}) %all-to-all-start.1) | async-done | bytes 6291488 | tf_op jit(solution)/shard_map/all_to_all | solution.py:15
  271.0 7.1 %all-to-all-start = ((bf16[8,192,512]{2,1,0:T(8,128)(2,1)}), bf16[8,192,512]{2,1,0:T(8,128)(2,1)S(1)}, u32[]{:S(2)}, u32[]{:S(2)}) async-start(bf16[8,192,512]{2,1,0:T(8,128)(2,1)} %bitcast), calls=%async_computation | async-start | bytes 3145728 | tf_op jit(solution)/shard_map/all_to_all | solution.py:15
  278.0 4.9 %reduce_sum.25 = bf16[48,2048]{1,0:T(8,128)(2,1)} reduce(bf16[32,48,2048]{2,1,0:T(8,128)(2,1)} %all-to-all-done.1, bf16[]{:T(256)} %constant.3.clone.1), dimensions={0}, to_apply=%region_1.0 | reduce | flops 3047424 | bytes 6488066 | tf_op jit(solution)/shard_map/reduce_sum | solution.py:16
  282.9 25.3 %all-to-all-done = bf16[8,192,512]{2,1,0:T(8,128)(2,1)S(1)} async-done(((bf16[8,192,512]{2,1,0:T(8,128)(2,1)}), bf16[8,192,512]{2,1,0:T(8,128)(2,1)S(1)}, u32[]{:S(2)}, u32[]{:S(2)}) %all-to-all-start) | async-done | bytes 1572896 | tf_op jit(solution)/shard_map/all_to_all | solution.py:15
  308.3 0.9 reduce_sum.24
Async XLA Ops:
  7.2 75.4 %all-gather.5.cloned.1.call-start = ((), (), s32[]{:S(2)}) async-start(), calls=%async_computation.3 | async-start | bytes 1769472 | tf_op jit(solution)/shard_map/all_gather | solution.py:28
  7.9 222.5 %all-gather.3.cloned.1.call-start = ((), (), s32[]{:S(2)}) async-start(), calls=%async_computation.2 | async-start | bytes 6488064 | tf_op jit(solution)/shard_map/all_gather | solution.py:22
  91.3 179.6 %all-to-all-start.1 = ((bf16[32,48,2048]{2,1,0:T(8,128)(2,1)}), bf16[32,48,2048]{2,1,0:T(8,128)(2,1)}, u32[]{:S(2)}, u32[]{:S(2)}) async-start(bf16[32,48,2048]{2,1,0:T(8,128)(2,1)} %bitcast.4), calls=%async_computation.1 | async-start | bytes 12582912 | tf_op jit(solution)/shard_map/all_to_all | solution.py:15
  271.0 37.3 %all-to-all-start = ((bf16[8,192,512]{2,1,0:T(8,128)(2,1)}), bf16[8,192,512]{2,1,0:T(8,128)(2,1)S(1)}, u32[]{:S(2)}, u32[]{:S(2)}) async-start(bf16[8,192,512]{2,1,0:T(8,128)(2,1)} %bitcast), calls=%async_computation | async-start | bytes 3145728 | tf_op jit(solution)/shard_map/all_to_all | solution.py:15
Sparse Core Ops, SparseCore 0:
  10.6 71.9 all-gather.4
  84.4 145.9 all-gather.2
where the time goes:
time: 316 us
  waiting for transfers between devices  266 us (84%)
  matrix products  17.4 us (6%)
  between operations  14 us (4%)
  starting transfers between devices  12.4 us (4%)
  other arithmetic  5.84 us (2%)
    all_gather x1, waiting for transfers between devices, local(): lax.all_gather(embed_second, 'row', axis=0, tiled=True)  134 us
    all_gather x1, waiting for transfers between devices, local(): whole_first = lax.all_gather(embed_first, 'col', axis=0, tiled=True)  73.9 us
    all_to_all x2, waiting for transfers between devices, sent_and_summed(): parts = lax.all_to_all(cut_along(x, dim, peers), axis, 0, 0, tiled=True)  57.3 us
    all_to_all x2, starting transfers between devices, sent_and_summed(): parts = lax.all_to_all(cut_along(x, dim, peers), axis, 0, 0, tiled=True)  12.3 us
    dot_general x1, matrix products, local(): jnp.dot(whole_first, low_grad, preferred_element_type=jnp.float32)  8.75 us
    dot_general x1, matrix products, local(): lax.dot_general(lax.all_gather(embed_second, 'row', axis=0, tiled=True),...  8.64 us
  transfers between devices with their start and end apart: 4, of which 4 were waited for; matrix products, arithmetic and copies ran while one was open for 7% of the time, Pallas kernels for 0%

commit v1 on v0

--- a/solution.py
+++ b/solution.py
@@ -25,7 +25,9 @@
         preferred_element_type=jnp.float32,
     )
     grad_first = sent_and_summed(first_terms.astype(jnp.bfloat16), "col", 0).astype(jnp.bfloat16)
-    whole_first = lax.all_gather(embed_first, "col", axis=0, tiled=True)
+    whole_first = jnp.concatenate(
+        lax.all_to_all(jnp.stack([embed_first] * lax.axis_size("col")), "col", 0, 0), axis=0
+    )
     grad_second = sent_and_summed(
         jnp.dot(whole_first, low_grad, preferred_element_type=jnp.float32).astype(jnp.bfloat16),
         "row",

time: 316 us -> 285 us (0.902)
  waiting for transfers between devices: 266 us -> 207 us
  starting transfers between devices: 12.4 us -> 37.4 us
    all_gather x1, waiting for transfers between devices: 134 us -> 51.7 us  [local(): lax.all_gather(embed_second, 'row', axis=0, tiled=True)]
    all_gather x1 -> x0, waiting for transfers between devices: 73.9 us -> none  [local(): whole_first = lax.all_gather(embed_first, 'col', axis=0, tiled=True)]
    all_to_all x2, waiting for transfers between devices: 57.3 us -> 116 us  [sent_and_summed(): parts = lax.all_to_all(cut_along(x, dim, peers), axis, 0, 0, tiled=True)]
    all_to_all x0 -> x1, waiting for transfers between devices: none -> 38.6 us  [local(): lax.all_to_all(jnp.stack([embed_first] * lax.axis_size('col')), 'col', 0, 0)]
    all_to_all x2, starting transfers between devices: 12.3 us -> 26.2 us  [sent_and_summed(): parts = lax.all_to_all(cut_along(x, dim, peers), axis, 0, 0, tiled=True)]
    all_to_all x0 -> x1, starting transfers between devices: none -> 11.1 us  [local(): lax.all_to_all(jnp.stack([embed_first] * lax.axis_size('col')), 'col', 0, 0)]
where the time goes in v1:
time: 285 us; the launch traced here: 282 us
  waiting for transfers between devices  207 us (73%)
  starting transfers between devices  37.4 us (13%)
  matrix products  16.1 us (6%)
  between operations  14 us (5%)
  other arithmetic  5.84 us (2%)
    all_to_all x2, waiting for transfers between devices, sent_and_summed(): parts = lax.all_to_all(cut_along(x, dim, peers), axis, 0, 0, tiled=True)  116 us
    all_gather x1, waiting for transfers between devices, local(): lax.all_gather(embed_second, 'row', axis=0, tiled=True)  51.7 us
    all_to_all x1, waiting for transfers between devices, local(): lax.all_to_all(jnp.stack([embed_first] * lax.axis_size('col')), 'col', 0, 0)  38.6 us
    all_to_all x2, starting transfers between devices, sent_and_summed(): parts = lax.all_to_all(cut_along(x, dim, peers), axis, 0, 0, tiled=True)  26.2 us
    all_to_all x1, starting transfers between devices, local(): lax.all_to_all(jnp.stack([embed_first] * lax.axis_size('col')), 'col', 0, 0)  11.1 us
    dot_general x1, matrix products, local(): lax.dot_general(lax.all_gather(embed_second, 'row', axis=0, tiled=True),...  8.64 us
    dot_general x1, matrix products, local(): jnp.dot(whole_first, low_grad, preferred_element_type=jnp.float32)  7.47 us
    reduce_sum x2, other arithmetic, sent_and_summed(): return jnp.sum(parts.astype(jnp.float32), axis=0)  5.84 us
  transfers between devices with their start and end apart: 4, of which 4 were waited for; matrix products, arithmetic and copies ran while one was open for 7% of the time, Pallas kernels for 0%

profile of v1, /device:TPU:2, one launch (start us, length us, event | category | flops | bytes accessed | tf_op | source)
XLA Modules:
  0.0 282.3 jit_solution(3234890773814586554)
XLA Ops:
  7.2 2.2 stack.2
  9.4 11.1 %all-to-all-start.1 = ((bf16[8,192,512]{2,1,0:T(8,128)(2,1)}), bf16[8,192,512]{2,1,0:T(8,128)(2,1)S(1)}, u32[]{:S(2)}, u32[]{:S(2)}) async-start(bf16[8,192,512]{2,1,0:T(8,128)(2,1)} %stack.2), calls=%async_computation.1 | async-start | bytes 3145728 | tf_op jit(solution)/shard_map/all_to_all | solution.py:29
  20.5 0.0 all-gather.2.cloned.1.call-start
  20.5 0.7 all-gather.2.cloned.1.call-update
  21.2 38.6 %all-to-all-done.1 = bf16[8,192,512]{2,1,0:T(8,128)(2,1)S(1)} async-done(((bf16[8,192,512]{2,1,0:T(8,128)(2,1)}), bf16[8,192,512]{2,1,0:T(8,128)(2,1)S(1)}, u32[]{:S(2)}, u32[]{:S(2)}) %all-to-all-start.1) | async-done | bytes 1572896 | tf_op jit(solution)/shard_map/all_to_all | solution.py:29
  59.8 7.5 %convolution_convert_fusion = bf16[1536,2048]{1,0:T(8,128)(2,1)} fusion(bf16[1536,512]{1,0:T(8,128)(2,1)S(1)} %bitcast.6, f32[512,2048]{1,0:T(8,128)} %param.5), kind=kOutput, calls=%fused_computation | convolution fusion | flops 3225419776 | bytes 12058624 | tf_op jit(solution)/shard_map/dot_general | solution.py:32
  67.2 19.0 %all-to-all-start.2 = ((bf16[32,48,2048]{2,1,0:T(8,128)(2,1)}), bf16[32,48,2048]{2,1,0:T(8,128)(2,1)}, u32[]{:S(2)}, u32[]{:S(2)}) async-start(bf16[32,48,2048]{2,1,0:T(8,128)(2,1)} %bitcast.5), calls=%async_computation.2 | async-start | bytes 12582912 | tf_op jit(solution)/shard_map/all_to_all | solution.py:15
  86.3 51.7 %all-gather.2.cloned.1.call-done = bf16[1536,2048]{1,0:T(8,128)(2,1)} async-done(((bf16[48,2048]{1,0:T(8,128)(2,1)}), bf16[1536,2048]{1,0:T(8,128)(2,1)}) %all-gather.2.cloned.1.call-update) | async-done | bytes 6291472 | tf_op jit(solution)/shard_map/all_gather | solution.py:22
  137.9 8.6 %convolution_convert_fusion.1 = bf16[1536,512]{1,0:T(8,128)(2,1)} fusion(bf16[1536,2048]{1,0:T(8,128)(2,1)} %all-gather.2.cloned.1.call-done, f32[512,2048]{1,0:T(8,128)} %param.5), kind=kOutput, calls=%fused_computation.1 | convolution fusion | flops 3223060480 | bytes 12058624 | tf_op jit(solution)/shard_map/dot_general | solution.py:21
  146.6 94.5 %all-to-all-done.2 = bf16[32,48,2048]{2,1,0:T(8,128)(2,1)} async-done(((bf16[32,48,2048]{2,1,0:T(8,128)(2,1)}), bf16[32,48,2048]{2,1,0:T(8,128)(2,1)}, u32[]{:S(2)}, u32[]{:S(2)}) %all-to-all-start.2) | async-done | bytes 6291488 | tf_op jit(solution)/shard_map/all_to_all | solution.py:15
  241.1 7.2 %all-to-all-start = ((bf16[8,192,512]{2,1,0:T(8,128)(2,1)}), bf16[8,192,512]{2,1,0:T(8,128)(2,1)S(1)}, u32[]{:S(2)}, u32[]{:S(2)}) async-start(bf16[8,192,512]{2,1,0:T(8,128)(2,1)} %bitcast), calls=%async_computation | async-start | bytes 3145728 | tf_op jit(solution)/shard_map/all_to_all | solution.py:15
  248.3 4.9 %reduce_sum.25 = bf16[48,2048]{1,0:T(8,128)(2,1)} reduce(bf16[32,48,2048]{2,1,0:T(8,128)(2,1)} %all-to-all-done.2, bf16[]{:T(256)} %constant.3.clone.1), dimensions={0}, to_apply=%region_1.0 | reduce | flops 3047424 | bytes 6488066 | tf_op jit(solution)/shard_map/reduce_sum | solution.py:16
  253.2 21.3 %all-to-all-done = bf16[8,192,512]{2,1,0:T(8,128)(2,1)S(1)} async-done(((bf16[8,192,512]{2,1,0:T(8,128)(2,1)}), bf16[8,192,512]{2,1,0:T(8,128)(2,1)S(1)}, u32[]{:S(2)}, u32[]{:S(2)}) %all-to-all-start) | async-done | bytes 1572896 | tf_op jit(solution)/shard_map/all_to_all | solution.py:15
  274.5 0.9 reduce_sum.24
Async XLA Ops:
  9.4 50.4 %all-to-all-start.1 = ((bf16[8,192,512]{2,1,0:T(8,128)(2,1)}), bf16[8,192,512]{2,1,0:T(8,128)(2,1)S(1)}, u32[]{:S(2)}, u32[]{:S(2)}) async-start(bf16[8,192,512]{2,1,0:T(8,128)(2,1)} %stack.2), calls=%async_computation.1 | async-start | bytes 3145728 | tf_op jit(solution)/shard_map/all_to_all | solution.py:29
  20.5 117.5 %all-gather.2.cloned.1.call-start = ((), (), s32[]{:S(2)}) async-start(), calls=%async_computation.3 | async-start | bytes 6488064 | tf_op jit(solution)/shard_map/all_gather | solution.py:22
  67.2 173.8 %all-to-all-start.2 = ((bf16[32,48,2048]{2,1,0:T(8,128)(2,1)}), bf16[32,48,2048]{2,1,0:T(8,128)(2,1)}, u32[]{:S(2)}, u32[]{:S(2)}) async-start(bf16[32,48,2048]{2,1,0:T(8,128)(2,1)} %bitcast.5), calls=%async_computation.2 | async-start | bytes 12582912 | tf_op jit(solution)/shard_map/all_to_all | solution.py:15
  241.1 33.5 %all-to-all-start = ((bf16[8,192,512]{2,1,0:T(8,128)(2,1)}), bf16[8,192,512]{2,1,0:T(8,128)(2,1)S(1)}, u32[]{:S(2)}, u32[]{:S(2)}) async-start(bf16[8,192,512]{2,1,0:T(8,128)(2,1)} %bitcast), calls=%async_computation | async-start | bytes 3145728 | tf_op jit(solution)/shard_map/all_to_all | solution.py:15
Sparse Core Ops, SparseCore 0:
  23.1 114.7 all-gather.1
